TPU v7x, 16 devices: a 4x2x1 block of a 4x4x8 slice. The times are simulated.
16 devices in a mesh: rep: 2 (over y, z), dp: 8 (over x, core).
Axes of the slice: x: 4, y: 2, z: 1, core: 2. Of those that a mesh axis runs over, the one named last changes fastest.
The devices are a block of a 4x4x8 slice.
Arguments:
- a: bfloat16 [16, 4, 4096, 1024], P(('rep', 'dp')), parts along dimension 0
- g: bfloat16 [16, 4, 4096, 2816], P(('rep', 'dp')), parts along dimension 0
Outputs:
- output: bfloat16 [8, 1024, 2816], P('rep'), parts along dimension 0
There are 2 independent parts. A program takes and returns all parts, laid end to end along the dimension named above; each array names one.
All inputs are finite; a program needn't handle non-finite values.
Results may differ from a plain program's by a relative error of at most 0.012.
Values are sent between devices in bfloat16 or wider.
A program may use at most 768 MiB of HBM per device.

v0:
```python
import jax
import jax.numpy as jnp


def solution(mesh):
    groups = mesh.shape["rep"]

    def step(a, g):
        a, g = (t.reshape(groups, -1, *t.shape[1:]) for t in (a, g))
        sums = jnp.einsum("rsntd,rsntf->rndf", a, g, preferred_element_type=jnp.float32)
        return sums.astype(jnp.bfloat16).reshape(-1, *sums.shape[2:])

    return step
```

profile of v0, /device:TPU:113, one launch (start us, length us, event | category | flops | bytes accessed | tf_op | source)
XLA Modules:
  0.0 577.9 jit_solution(8767886110147109727)
XLA Ops:
  0.0 114.9 %fusion.3 = f32[1,4,1024,2816]{3,2,1,0:T(8,128)} fusion(bf16[1,4,4096,2816]{3,2,1,0:T(8,128)(2,1)} %param.1, bf16[1,4,4096,1024]{3,2,1,0:T(8,128)(2,1)} %param), kind=kOutput, calls=%fused_computation.3 | convolution fusion | flops 94489280512 | bytes 171966464 | tf_op jit(solution)/rsntd,rsntf->rndf/dot_general | solution.py:10
  114.9 463.0 %all-reduce.2 = bf16[1,4,1024,2816]{3,2,1,0:T(8,128)(2,1)} all-reduce(f32[1,4,1024,2816]{3,2,1,0:T(8,128)} %fusion.3), channel_id=1, replica_groups=[2,8]<=[16], use_global_device_ids=true, to_apply=%add.clone | all-reduce | flops 11534336 | bytes 69206016 | tf_op jit(solution)/rsntd,rsntf->rndf/dot_general | solution.py:10
where the time goes:
time: 580 us; the launch traced here: 578 us
  blocking collectives  463 us (80%)
  matrix products  115 us (20%)
    dot_general x1, blocking collectives, step(): jnp.einsum('rsntd,rsntf->rndf', a, g, preferred_element_type=jnp.float32)  463 us
    dot_general x1, matrix products, step(): jnp.einsum('rsntd,rsntf->rndf', a, g, preferred_element_type=jnp.float32)  115 us

commit v1 on v0

v1 whole, which is shorter than its diff:
```python
import functools

import jax
import jax.numpy as jnp
from jax import lax
from jax.experimental import pallas as pl
from jax.experimental.pallas import tpu as pltpu
from jax.sharding import PartitionSpec as P

MESH = pl.DeviceIdType.MESH
WIDTH = 256
CORES = 2
LAG = (1, 3, 5)
EVERY = 4
FORWARD, LAST = 3, 6
SLOTS = 8
SWAPS = 4
DEEP = 3
F32 = jnp.float32
CONTRACT = (((0,), (0,)), ((), ()))


def kernel(chips, a_hbm, g_hbm, out, a_buf, g_buf, acc, own, swap, sends, lands,
           a_sem, g_sem, swap_send, swap_recv, send_sem, recv_sem, hop_send, gather_recv, across_send, across_recv):
    matrices = a_hbm.shape[1]
    chunks, rows, width = out.shape
    per = chunks // matrices
    half = rows // CORES
    block = half // chips
    kept = own.shape[0]

    rep, me = lax.axis_index("rep"), lax.axis_index("dp")
    chip, core = me // CORES, lax.rem(me, CORES)
    sign = 1 - 2 * core
    ahead = lax.rem(chip + sign + chips, chips)
    behind = lax.rem(chip - sign + chips, chips)
    opposite = lax.rem(chip + 2, chips)
    to_ahead, to_behind = (rep, ahead * CORES + core), (rep, behind * CORES + core)
    to_other = (rep, chip * CORES + 1 - core)

    barrier = pltpu.get_barrier_semaphore()
    for device in (to_ahead, to_behind, to_other):
        pl.semaphore_signal(barrier, inc=1, device_id=device, device_id_type=MESH)
    pl.semaphore_wait(barrier, 3)

    def remote(src, dst, send, recv, device):
        return pltpu.make_async_remote_copy(
            src_ref=src, dst_ref=dst, send_sem=send, recv_sem=recv, device_id=device, device_id_type=MESH
        )

    def a_copy(n):
        slot = lax.rem(n, 2)
        return pltpu.make_async_copy(a_hbm.at[0, n], a_buf.at[slot], a_sem.at[slot])

    def g_copy(u):
        slot = lax.rem(u, DEEP)
        columns = pl.ds(pl.multiple_of(lax.rem(u, per) * width, width), width)
        return pltpu.make_async_copy(g_hbm.at[0, u // per, :, columns], g_buf.at[slot], g_sem.at[slot])

    def in_half(b):
        return pl.ds(pl.multiple_of(b * block, block), block)

    def in_chunk(b):
        return pl.ds(pl.multiple_of(core * half + b * block, block), block)

    mine = pl.ds(pl.multiple_of(core * half, half), half)
    others = pl.ds(pl.multiple_of((1 - core) * half, half), half)

    def swap_copy(u):
        slot = lax.rem(u, SWAPS)
        return remote(swap.at[slot], out.at[u, others], swap_send.at[slot], swap_recv.at[u], to_other)

    def reduce_copy(kind, u, device):
        slot = lax.rem(u, SLOTS)
        return remote(sends.at[kind, slot], lands.at[kind, u], send_sem.at[kind, slot], recv_sem.at[kind, u], device)

    first = functools.partial(reduce_copy, 0, device=to_ahead)
    second = functools.partial(reduce_copy, 1, device=to_ahead)
    direct = functools.partial(reduce_copy, 2, device=to_behind)

    def gather_copy(kind, u, b, device):
        piece = out.at[u, in_chunk(b)]
        return remote(piece, piece, hop_send, gather_recv.at[kind, u], device)

    def across(u, b):
        piece = out.at[u, in_chunk(b)]
        return remote(piece, piece, across_send, across_recv, to_other)

    def multiply(u):
        n = u // per
        slot = lax.rem(u, DEEP)

        @pl.when(lax.rem(u, per) == 0)
        def _():
            a_copy(n).wait()

            @pl.when(n + 1 < matrices)
            def _():
                a_copy(n + 1).start()

        @pl.when(u + DEEP - 1 < chunks)
        def _():
            g_copy(u + DEEP - 1).start()

        g_copy(u).wait()
        acc[...] = lax.dot_general(a_buf[lax.rem(n, 2)], g_buf[slot], CONTRACT, preferred_element_type=F32)

        @pl.when(u >= SWAPS)
        def _():
            swap_copy(u - SWAPS).wait_send()

        swap[lax.rem(u, SWAPS)] = acc[others, :].astype(swap.dtype)
        swap_copy(u).start()
        own[lax.rem(u, kept)] = acc[mine, :]

    def of_chip(u, b):
        return own[lax.rem(u, kept), in_half(b), :] + out[u, in_chunk(b), :].astype(F32)

    def put(kind, u, value):
        sends[kind, lax.rem(u, SLOTS)] = value.astype(sends.dtype)

    def free(copy, u):
        @pl.when(u >= SLOTS)
        def _():
            copy(u - SLOTS).wait_send()

    def stage_1(u):
        swap_copy(u).wait_recv()
        free(first, u)
        put(0, u, of_chip(u, opposite))
        first(u).start()
        free(direct, u)
        put(2, u, of_chip(u, behind))
        direct(u).start()

    def stage_2(u):
        first(u).wait_recv()
        free(second, u)
        put(1, u, of_chip(u, ahead) + lands[0, u].astype(F32))
        second(u).start()

    def stage_3(u):
        second(u).wait_recv()
        direct(u).wait_recv()
        total = of_chip(u, chip) + lands[1, u].astype(F32) + lands[2, u].astype(F32)
        out[u, in_chunk(chip), :] = total.astype(out.dtype)

    stages = (stage_1, stage_2, stage_3)

    def gather(k):
        @pl.when(k < chunks)
        def _():
            gather_copy(0, k, chip, to_ahead).start()
            gather_copy(1, k, chip, to_behind).start()
            across(k, chip).start()

        @pl.when((k >= FORWARD) & (k < chunks + FORWARD))
        def _():
            u = k - FORWARD
            gather_copy(0, u, behind, to_ahead).wait_recv()
            gather_copy(2, u, behind, to_ahead).start()
            across(u, behind).start()
            gather_copy(1, u, ahead, to_behind).wait_recv()
            across(u, ahead).start()

        @pl.when((k >= LAST) & (k < chunks + LAST))
        def _():
            u = k - LAST
            gather_copy(2, u, opposite, to_ahead).wait_recv()
            across(u, opposite).start()

    a_copy(0).start()
    for u in range(DEEP - 1):
        g_copy(u).start()

    begin = LAG[-1] + 1
    early = (chunks - begin + EVERY - 1) // EVERY

    @pl.loop(0, chunks)
    def _(s):
        multiply(s)
        for stage, lag in zip(stages, LAG):
            pl.when(s >= lag)(functools.partial(stage, s - lag))
        pl.when((s >= begin) & (lax.rem(s - begin, EVERY) == 0))(lambda: gather((s - begin) // EVERY))

    @pl.loop(0, LAG[-1])
    def _(t):
        for stage, lag in zip(stages, LAG):
            pl.when(t < lag)(functools.partial(stage, t + chunks - lag))
        gather(t + early)

    @pl.loop(early + LAG[-1], chunks + LAST)
    def _(k):
        gather(k)

    @pl.loop(chunks - SLOTS, chunks)
    def _(u):
        for copy in (first, second, direct):
            copy(u).wait_send()

    @pl.loop(chunks - SWAPS, chunks)
    def _(u):
        swap_copy(u).wait_send()

    three = out.at[:, pl.ds(0, 3 * block)]
    remote(three, three, hop_send, across_recv, to_ahead).wait_send()
    remote(out.at[:, mine], out.at[:, others], across_send, across_recv, to_other).wait()


def place(per, sums, out, sem):
    chunks, _, width = sums.shape

    def copy(u):
        columns = pl.ds(pl.multiple_of(lax.rem(u, per) * width, width), width)
        return pltpu.make_async_copy(sums.at[u], out.at[u // per, :, columns], sem.at[u])

    @pl.loop(0, chunks)
    def _(u):
        copy(u).start()

    @pl.loop(0, chunks)
    def _(u):
        copy(u).wait()


def solution(mesh):
    chips = mesh.shape["dp"] // CORES

    def step(a, g):
        _, matrices, tokens, rows = a.shape
        columns = g.shape[3]
        width, dtype = WIDTH, a.dtype
        per = columns // width
        chunks = matrices * per
        half = rows // CORES
        block = half // chips
        flops = 2 * matrices * tokens * rows * columns
        sems = pltpu.SemaphoreType.DMA
        sums = pl.pallas_call(
            functools.partial(kernel, chips),
            name="multiply_and_sum",
            out_shape=pltpu.VMEM((chunks, rows, width), dtype),
            in_specs=[pl.BlockSpec(memory_space=pl.ANY)] * 2,
            out_specs=pl.BlockSpec(memory_space=pltpu.VMEM),
            scratch_shapes=[
                pltpu.VMEM((2, tokens, rows), dtype),
                pltpu.VMEM((DEEP, tokens, width), dtype),
                pltpu.VMEM((rows, width), F32),
                pltpu.VMEM((LAG[-1] + 1, half, width), F32),
                pltpu.VMEM((SWAPS, half, width), dtype),
                pltpu.VMEM((3, SLOTS, block, width), dtype),
                pltpu.VMEM((3, chunks, block, width), dtype),
                sems((2,)),
                sems((DEEP,)),
                sems((SWAPS,)),
                sems((chunks,)),
                sems((3, SLOTS)),
                sems((3, chunks)),
                sems,
                sems((3, chunks)),
                sems,
                sems,
            ],
            compiler_params=pltpu.CompilerParams(
                collective_id=0, has_side_effects=True, vmem_limit_bytes=40 * 2**20
            ),
            cost_estimate=pl.CostEstimate(flops=flops, bytes_accessed=2 * (a.size + g.size), transcendentals=0),
        )(a, g)
        return pl.pallas_call(
            functools.partial(place, per),
            name="place",
            out_shape=jax.ShapeDtypeStruct((matrices, rows, columns), dtype),
            in_specs=[pl.BlockSpec(memory_space=pltpu.VMEM)],
            out_specs=pl.BlockSpec(memory_space=pl.ANY),
            scratch_shapes=[sems((chunks,))],
            compiler_params=pltpu.CompilerParams(vmem_limit_bytes=2**20),
        )(sums)

    return jax.shard_map(
        step,
        mesh=mesh,
        in_specs=(P(("rep", "dp")), P(("rep", "dp"))),
        out_specs=P("rep"),
        check_vma=False,
    )
```

time: 580 us -> 225 us (0.39)
  blocking collectives: 463 us -> 0 us
  Pallas kernels: 0 us -> 225 us
  matrix products: 115 us -> 0 us
    dot_general x1 -> x0, blocking collectives: 463 us -> none  [step(): jnp.einsum('rsntd,rsntf->rndf', a, g, preferred_element_type=jnp.float32)]
    pallas_call x0 -> x2, Pallas kernels: none -> 225 us  [the longest x1 217 us: step(): pl.pallas_call(functools.partial(kernel, chips), name='multiply_and_sum',...]
    dot_general x1 -> x0, matrix products: 115 us -> none  [step(): jnp.einsum('rsntd,rsntf->rndf', a, g, preferred_element_type=jnp.float32)]
where the time goes in v1:
time: 225 us
  Pallas kernels  225 us (100%)
    pallas_call x1, Pallas kernels, step(): pl.pallas_call(functools.partial(kernel, chips), name='multiply_and_sum',...  217 us
    pallas_call x1, Pallas kernels, step(): pl.pallas_call(functools.partial(place, per), name='place', out_shape=jax...  8.08 us

profile of v1, /device:TPU:113, one launch (start us, length us, event | category | flops | bytes accessed | tf_op | source)
XLA Modules:
  0.0 224.7 jit_solution(8470136678274339304)
XLA Ops:
  0.0 216.6 %multiply_and_sum.1.sums = bf16[44,1024,256]{2,1,0:T(8,128)(2,1)S(1)} custom-call(bf16[1,4,4096,1024]{3,2,1,0:T(8,128)(2,1)} %a_hbm.1, bf16[1,4,4096,2816]{3,2,1,0:T(8,128)(2,1)} %g_hbm.1), custom_call_target="tpu_custom_call" | custom-call | flops 94489280512 | bytes 125829120 | tf_op jit(solution)/shard_map/multiply_and_sum/pallas_call | solution.py:239
  216.6 8.1 %place.1 = bf16[4,1024,2816]{2,1,0:T(8,128)(2,1)} custom-call(bf16[44,1024,256]{2,1,0:T(8,128)(2,1)S(1)} %multiply_and_sum.1.sums), custom_call_target="tpu_custom_call" | custom-call | tf_op jit(solution)/shard_map/place/pallas_call | solution.py:269

commit v2 on v1

--- a/solution.py
+++ b/solution.py
@@ -10,9 +10,12 @@
 MESH = pl.DeviceIdType.MESH
 WIDTH = 256
 CORES = 2
-LAG = (1, 3, 5)
-EVERY = 4
+HALVED, TURN = 4, 8
+FIRST, SECOND, THIRD = ((0, 0), (HALVED, 1)), ((0, 1), (HALVED, 2), (TURN, 3)), ((0, 2), (HALVED, 3), (TURN, 5))
+EVERY = 2
 FORWARD, LAST = 3, 6
+TURNS = 12
+PARTS = 4
 SLOTS = 8
 SWAPS = 4
 DEEP = 3
@@ -20,14 +23,23 @@
 CONTRACT = (((0,), (0,)), ((), ()))
 
 
+def late(s, lag, limit):
+    due, u = False, 0
+    for (n, steps), end in zip(lag, [n for n, _ in lag[1:]] + [limit]):
+        here = (s - steps >= n) & (s - steps < end)
+        due, u = due | here, jnp.where(here, s - steps, u)
+    return due, u
+
+
 def kernel(chips, a_hbm, g_hbm, out, a_buf, g_buf, acc, own, swap, sends, lands,
-           a_sem, g_sem, swap_send, swap_recv, send_sem, recv_sem, hop_send, gather_recv, across_send, across_recv):
+           part_sem, a_sem, g_sem, swap_send, swap_recv, send_sem, recv_sem, hop_send, gather_recv, across_send, across_recv):
     matrices = a_hbm.shape[1]
     chunks, rows, width = out.shape
     per = chunks // matrices
     half = rows // CORES
     block = half // chips
     kept = own.shape[0]
+    depth = a_buf.shape[1] // PARTS
 
     rep, me = lax.axis_index("rep"), lax.axis_index("dp")
     chip, core = me // CORES, lax.rem(me, CORES)
@@ -41,7 +53,6 @@
     barrier = pltpu.get_barrier_semaphore()
     for device in (to_ahead, to_behind, to_other):
         pl.semaphore_signal(barrier, inc=1, device_id=device, device_id_type=MESH)
-    pl.semaphore_wait(barrier, 3)
 
     def remote(src, dst, send, recv, device):
         return pltpu.make_async_remote_copy(
@@ -68,11 +79,11 @@
 
     def swap_copy(u):
         slot = lax.rem(u, SWAPS)
-        return remote(swap.at[slot], out.at[u, others], swap_send.at[slot], swap_recv.at[u], to_other)
+        return remote(swap.at[slot], out.at[u, others], swap_send.at[slot], swap_recv.at[lax.rem(u, TURNS)], to_other)
 
     def reduce_copy(kind, u, device):
         slot = lax.rem(u, SLOTS)
-        return remote(sends.at[kind, slot], lands.at[kind, u], send_sem.at[kind, slot], recv_sem.at[kind, u], device)
+        return remote(sends.at[kind, slot], lands.at[kind, u], send_sem.at[kind, slot], recv_sem.at[kind, lax.rem(u, TURNS)], device)
 
     first = functools.partial(reduce_copy, 0, device=to_ahead)
     second = functools.partial(reduce_copy, 1, device=to_ahead)
@@ -80,38 +91,87 @@
 
     def gather_copy(kind, u, b, device):
         piece = out.at[u, in_chunk(b)]
-        return remote(piece, piece, hop_send, gather_recv.at[kind, u], device)
+        return remote(piece, piece, hop_send, gather_recv.at[kind, lax.rem(u, TURNS)], device)
 
     def across(u, b):
         piece = out.at[u, in_chunk(b)]
         return remote(piece, piece, across_send, across_recv, to_other)
 
-    def multiply(u):
+    def dot(a, g):
+        return lax.dot_general(a, g, CONTRACT, preferred_element_type=F32)
+
+    def quarters(h):
+        part = half // 2
+        for q in range(2):
+            yield pl.ds(q * part, part), pl.ds(pl.multiple_of(h * half + q * part, part), part)
+
+    def multiply(u, halved):
         n = u // per
-        slot = lax.rem(u, DEEP)
 
         @pl.when(lax.rem(u, per) == 0)
         def _():
             a_copy(n).wait()
 
-            @pl.when(n + 1 < matrices)
+        @pl.when((lax.rem(u, per) == 1) & (n + 1 < matrices))
+        def _():
+            a_copy(n + 1).start()
+
+        @pl.when(u + DEEP - 1 < chunks)
+        def _():
+            g_copy(u + DEEP - 1).start()
+
+        @pl.when(u >= SWAPS)
+        def _():
+            swap_copy(u - SWAPS).wait_send()
+
+        g_copy(u).wait()
+        if halved:
+            for to, at in quarters(1 - core):
+                value = dot(a_buf[lax.rem(n, 2), :, at], g_buf[lax.rem(u, DEEP)])
+                swap[lax.rem(u, SWAPS), to] = value.astype(swap.dtype)
+            swap_copy(u).start()
+            for to, at in quarters(core):
+                own[lax.rem(u, kept), to] = dot(a_buf[lax.rem(n, 2), :, at], g_buf[lax.rem(u, DEEP)])
+            return
+
+        for c in range(CORES):
+
+            @pl.when(core == c)
             def _():
-                a_copy(n + 1).start()
-
-        @pl.when(u + DEEP - 1 < chunks)
-        def _():
-            g_copy(u + DEEP - 1).start()
-
-        g_copy(u).wait()
-        acc[...] = lax.dot_general(a_buf[lax.rem(n, 2)], g_buf[slot], CONTRACT, preferred_element_type=F32)
-
-        @pl.when(u >= SWAPS)
-        def _():
-            swap_copy(u - SWAPS).wait_send()
-
-        swap[lax.rem(u, SWAPS)] = acc[others, :].astype(swap.dtype)
+                value = dot(a_buf[lax.rem(n, 2)], g_buf[lax.rem(u, DEEP)])
+                halves = [value[h * half : (h + 1) * half] for h in range(CORES)]
+                swap[lax.rem(u, SWAPS)] = halves[1 - c].astype(swap.dtype)
+                own[lax.rem(u, kept)] = halves[c]
+
         swap_copy(u).start()
-        own[lax.rem(u, kept)] = acc[mine, :]
+
+    def part_copy(kind, p):
+        tokens = pl.ds(p * depth, depth)
+        if kind == 2:
+            columns = pl.ds(0, width)
+            return pltpu.make_async_copy(g_hbm.at[0, 0, tokens, columns], g_buf.at[0, tokens], part_sem.at[kind, p])
+        columns = mine if kind else others
+        return pltpu.make_async_copy(
+            a_hbm.at[0, 0, tokens, columns], a_buf.at[0, tokens, columns], part_sem.at[kind, p]
+        )
+
+    def multiply_first():
+        for p in range(PARTS):
+            tokens = pl.ds(p * depth, depth)
+            part_copy(0, p).wait()
+            part_copy(2, p).wait()
+            for to, at in quarters(1 - core):
+                value = dot(a_buf[0, tokens, at], g_buf[0, tokens])
+                acc[to] = acc[to] + value if p else value
+        swap[0] = acc[...].astype(swap.dtype)
+        pl.semaphore_wait(barrier, 3)
+        swap_copy(0).start()
+        for p in range(PARTS):
+            tokens = pl.ds(p * depth, depth)
+            part_copy(1, p).wait()
+            for to, at in quarters(core):
+                value = dot(a_buf[0, tokens, at], g_buf[0, tokens])
+                own[0, to] = own[0, to] + value if p else value
 
     def of_chip(u, b):
         return own[lax.rem(u, kept), in_half(b), :] + out[u, in_chunk(b), :].astype(F32)
@@ -145,7 +205,8 @@
         total = of_chip(u, chip) + lands[1, u].astype(F32) + lands[2, u].astype(F32)
         out[u, in_chunk(chip), :] = total.astype(out.dtype)
 
-    stages = (stage_1, stage_2, stage_3)
+    def when(due, act):
+        pl.when(due[0])(lambda: act(due[1]))
 
     def gather(k):
         @pl.when(k < chunks)
@@ -169,27 +230,42 @@
             gather_copy(2, u, opposite, to_ahead).wait_recv()
             across(u, opposite).start()
 
-    a_copy(0).start()
-    for u in range(DEEP - 1):
+    for p in range(PARTS):
+        part_copy(2, p).start()
+        part_copy(0, p).start()
+    for p in range(PARTS):
+        part_copy(1, p).start()
+    for u in range(1, DEEP):
         g_copy(u).start()
-
-    begin = LAG[-1] + 1
-    early = (chunks - begin + EVERY - 1) // EVERY
-
-    @pl.loop(0, chunks)
-    def _(s):
-        multiply(s)
-        for stage, lag in zip(stages, LAG):
-            pl.when(s >= lag)(functools.partial(stage, s - lag))
-        pl.when((s >= begin) & (lax.rem(s - begin, EVERY) == 0))(lambda: gather((s - begin) // EVERY))
-
-    @pl.loop(0, LAG[-1])
+    multiply_first()
+    stage_1(0)
+
+    later = THIRD[-1][1]
+    settled = TURN + later
+    early = TURN + (chunks - settled + EVERY - 1) // EVERY
+
+    def reduce(s):
+        when(late(s, FIRST, chunks), stage_1)
+        when(late(s, SECOND, chunks), stage_2)
+        when(late(s, THIRD, chunks), stage_3)
+
+    def step(s, halved):
+        multiply(s, halved)
+        reduce(s)
+        due, k = late(s, THIRD[:-1], TURN)
+        after = s >= settled
+        due = due | (after & (lax.rem(s - settled, EVERY) == 0))
+        when((due, jnp.where(after, TURN + (s - settled) // EVERY, k)), gather)
+
+    pl.loop(1, HALVED)(functools.partial(step, halved=True))
+    pl.loop(HALVED, chunks)(functools.partial(step, halved=False))
+
+    @pl.loop(0, later)
     def _(t):
-        for stage, lag in zip(stages, LAG):
-            pl.when(t < lag)(functools.partial(stage, t + chunks - lag))
+        reduce(t + chunks)
         gather(t + early)
 
-    @pl.loop(early + LAG[-1], chunks + LAST)
+    @pl.loop(early + later, chunks + LAST)
     def _(k):
         gather(k)
 
@@ -245,19 +321,20 @@
             scratch_shapes=[
                 pltpu.VMEM((2, tokens, rows), dtype),
                 pltpu.VMEM((DEEP, tokens, width), dtype),
-                pltpu.VMEM((rows, width), F32),
-                pltpu.VMEM((LAG[-1] + 1, half, width), F32),
+                pltpu.VMEM((half, width), F32),
+                pltpu.VMEM((THIRD[-1][1] + 1, half, width), F32),
                 pltpu.VMEM((SWAPS, half, width), dtype),
                 pltpu.VMEM((3, SLOTS, block, width), dtype),
                 pltpu.VMEM((3, chunks, block, width), dtype),
+                sems((3, PARTS)),
                 sems((2,)),
                 sems((DEEP,)),
                 sems((SWAPS,)),
-                sems((chunks,)),
+                sems((TURNS,)),
                 sems((3, SLOTS)),
-                sems((3, chunks)),
+                sems((3, TURNS)),
                 sems,
-                sems((3, chunks)),
+                sems((3, TURNS)),
                 sems,
                 sems,
             ],

time: 225 us -> 213 us (0.947)
  Pallas kernels: 225 us -> 213 us
    pallas_call x1, Pallas kernels: 217 us -> 205 us  [step(): pl.pallas_call(functools.partial(kernel, chips), name='multiply_and_sum',...]
where the time goes in v2:
time: 213 us
  Pallas kernels  213 us (100%)
    pallas_call x1, Pallas kernels, step(): pl.pallas_call(functools.partial(kernel, chips), name='multiply_and_sum',...  205 us
    pallas_call x1, Pallas kernels, step(): pl.pallas_call(functools.partial(place, per), name='place', out_shape=jax...  8.08 us

profile of v2, /device:TPU:113, one launch (start us, length us, event | category | flops | bytes accessed | tf_op | source)
XLA Modules:
  0.0 213.2 jit_solution(2605481223130056983)
XLA Ops:
  0.0 204.9 %multiply_and_sum.1.sums = bf16[44,1024,256]{2,1,0:T(8,128)(2,1)S(1)} custom-call(bf16[1,4,4096,1024]{3,2,1,0:T(8,128)(2,1)} %a_hbm.1, bf16[1,4,4096,2816]{3,2,1,0:T(8,128)(2,1)} %g_hbm.1), custom_call_target="tpu_custom_call" | custom-call | flops 94489280512 | bytes 125829120 | tf_op jit(solution)/shard_map/multiply_and_sum/pallas_call | solution.py:315
  204.9 8.1 %place.1 = bf16[4,1024,2816]{2,1,0:T(8,128)(2,1)} custom-call(bf16[44,1024,256]{2,1,0:T(8,128)(2,1)S(1)} %multiply_and_sum.1.sums), custom_call_target="tpu_custom_call" | custom-call | tf_op jit(solution)/shard_map/place/pallas_call | solution.py:346

commit v3 on v2

--- a/solution.py
+++ b/solution.py
@@ -10,13 +10,13 @@
 MESH = pl.DeviceIdType.MESH
 WIDTH = 256
 CORES = 2
-HALVED, TURN = 4, 8
-FIRST, SECOND, THIRD = ((0, 0), (HALVED, 1)), ((0, 1), (HALVED, 2), (TURN, 3)), ((0, 2), (HALVED, 3), (TURN, 5))
+SECOND, THIRD = ((0, 1), (8, 2)), ((0, 3), (8, 4))
+TURN = 12
 EVERY = 2
 FORWARD, LAST = 3, 6
-TURNS = 12
+TURNS = 10
 PARTS = 4
-SLOTS = 8
+SLOTS = 6
 SWAPS = 4
 DEEP = 3
 F32 = jnp.float32
@@ -105,7 +105,7 @@
         for q in range(2):
             yield pl.ds(q * part, part), pl.ds(pl.multiple_of(h * half + q * part, part), part)
 
-    def multiply(u, halved):
+    def multiply(u):
         n = u // per
 
         @pl.when(lax.rem(u, per) == 0)
@@ -125,25 +125,12 @@
             swap_copy(u - SWAPS).wait_send()
 
         g_copy(u).wait()
-        if halved:
-            for to, at in quarters(1 - core):
-                value = dot(a_buf[lax.rem(n, 2), :, at], g_buf[lax.rem(u, DEEP)])
-                swap[lax.rem(u, SWAPS), to] = value.astype(swap.dtype)
-            swap_copy(u).start()
-            for to, at in quarters(core):
-                own[lax.rem(u, kept), to] = dot(a_buf[lax.rem(n, 2), :, at], g_buf[lax.rem(u, DEEP)])
-            return
-
-        for c in range(CORES):
-
-            @pl.when(core == c)
-            def _():
-                value = dot(a_buf[lax.rem(n, 2)], g_buf[lax.rem(u, DEEP)])
-                halves = [value[h * half : (h + 1) * half] for h in range(CORES)]
-                swap[lax.rem(u, SWAPS)] = halves[1 - c].astype(swap.dtype)
-                own[lax.rem(u, kept)] = halves[c]
-
+        for to, at in quarters(1 - core):
+            value = dot(a_buf[lax.rem(n, 2), :, at], g_buf[lax.rem(u, DEEP)])
+            swap[lax.rem(u, SWAPS), to] = value.astype(swap.dtype)
         swap_copy(u).start()
+        for to, at in quarters(core):
+            own[lax.rem(u, kept), to] = dot(a_buf[lax.rem(n, 2), :, at], g_buf[lax.rem(u, DEEP)])
 
     def part_copy(kind, p):
         tokens = pl.ds(p * depth, depth)
@@ -245,20 +232,18 @@
     early = TURN + (chunks - settled + EVERY - 1) // EVERY
 
     def reduce(s):
-        when(late(s, FIRST, chunks), stage_1)
+        pl.when(s < chunks)(lambda: stage_1(s))
         when(late(s, SECOND, chunks), stage_2)
         when(late(s, THIRD, chunks), stage_3)
 
-    def step(s, halved):
-        multiply(s, halved)
+    @pl.loop(1, chunks)
+    def _(s):
+        multiply(s)
         reduce(s)
-        due, k = late(s, THIRD[:-1], TURN)
+        due, k = late(s, THIRD, TURN)
         after = s >= settled
         due = due | (after & (lax.rem(s - settled, EVERY) == 0))
         when((due, jnp.where(after, TURN + (s - settled) // EVERY, k)), gather)
-
-    pl.loop(1, HALVED)(functools.partial(step, halved=True))
-    pl.loop(HALVED, chunks)(functools.partial(step, halved=False))
 
     @pl.loop(0, later)
     def _(t):

time: 213 us -> 211 us (level)
    pallas_call x1, Pallas kernels: 205 us -> 202 us  [step(): pl.pallas_call(functools.partial(kernel, chips), name='multiply_and_sum',...]
where the time goes in v3:
time: 211 us
  Pallas kernels  211 us (100%)
    pallas_call x1, Pallas kernels, step(): pl.pallas_call(functools.partial(kernel, chips), name='multiply_and_sum',...  202 us
    pallas_call x1, Pallas kernels, step(): pl.pallas_call(functools.partial(place, per), name='place', out_shape=jax...  8.08 us

profile of v3, /device:TPU:113, one launch (start us, length us, event | category | flops | bytes accessed | tf_op | source)
XLA Modules:
  0.0 210.6 jit_solution(15529061259612251305)
XLA Ops:
  0.0 202.5 %multiply_and_sum.1.sums = bf16[44,1024,256]{2,1,0:T(8,128)(2,1)S(1)} custom-call(bf16[1,4,4096,1024]{3,2,1,0:T(8,128)(2,1)} %a_hbm.1, bf16[1,4,4096,2816]{3,2,1,0:T(8,128)(2,1)} %g_hbm.1), custom_call_target="tpu_custom_call" | custom-call | flops 94489280512 | bytes 125829120 | tf_op jit(solution)/shard_map/multiply_and_sum/pallas_call | solution.py:300
  202.5 8.1 %place.1 = bf16[4,1024,2816]{2,1,0:T(8,128)(2,1)} custom-call(bf16[44,1024,256]{2,1,0:T(8,128)(2,1)S(1)} %multiply_and_sum.1.sums), custom_call_target="tpu_custom_call" | custom-call | tf_op jit(solution)/shard_map/place/pallas_call | solution.py:331

commit v4 on v3

--- a/solution.py
+++ b/solution.py
@@ -10,7 +10,7 @@
 MESH = pl.DeviceIdType.MESH
 WIDTH = 256
 CORES = 2
-SECOND, THIRD = ((0, 1), (8, 2)), ((0, 3), (8, 4))
+SECOND, THIRD = ((0, 1), (8, 2)), ((0, 3), (8, 5))
 TURN = 12
 EVERY = 2
 FORWARD, LAST = 3, 6
@@ -105,7 +105,7 @@
         for q in range(2):
             yield pl.ds(q * part, part), pl.ds(pl.multiple_of(h * half + q * part, part), part)
 
-    def multiply(u):
+    def multiply(u, between):
         n = u // per
 
         @pl.when(lax.rem(u, per) == 0)
@@ -129,6 +129,7 @@
             value = dot(a_buf[lax.rem(n, 2), :, at], g_buf[lax.rem(u, DEEP)])
             swap[lax.rem(u, SWAPS), to] = value.astype(swap.dtype)
         swap_copy(u).start()
+        between()
         for to, at in quarters(core):
             own[lax.rem(u, kept), to] = dot(a_buf[lax.rem(n, 2), :, at], g_buf[lax.rem(u, DEEP)])
 
@@ -234,19 +235,25 @@
     def reduce(s):
         pl.when(s < chunks)(lambda: stage_1(s))
         when(late(s, SECOND, chunks), stage_2)
+
+    def finish(s):
         when(late(s, THIRD, chunks), stage_3)
 
-    @pl.loop(1, chunks)
-    def _(s):
-        multiply(s)
-        reduce(s)
+    def between(s):
+        finish(s)
         due, k = late(s, THIRD, TURN)
         after = s >= settled
         due = due | (after & (lax.rem(s - settled, EVERY) == 0))
         when((due, jnp.where(after, TURN + (s - settled) // EVERY, k)), gather)
 
+    @pl.loop(1, chunks)
+    def _(s):
+        multiply(s, functools.partial(between, s))
+        reduce(s)
+
     @pl.loop(0, later)
     def _(t):
+        finish(t + chunks)
         reduce(t + chunks)
         gather(t + early)
 

time: 211 us -> 210 us (level)
  no operation moved by 1% of the time
where the time goes in v4:
time: 210 us
  Pallas kernels  210 us (100%)
    pallas_call x1, Pallas kernels, step(): pl.pallas_call(functools.partial(kernel, chips), name='multiply_and_sum',...  202 us
    pallas_call x1, Pallas kernels, step(): pl.pallas_call(functools.partial(place, per), name='place', out_shape=jax...  8.08 us

profile of v4, /device:TPU:113, one launch (start us, length us, event | category | flops | bytes accessed | tf_op | source)
XLA Modules:
  0.0 210.1 jit_solution(496037056502269721)
XLA Ops:
  0.0 202.0 %multiply_and_sum.1.sums = bf16[44,1024,256]{2,1,0:T(8,128)(2,1)S(1)} custom-call(bf16[1,4,4096,1024]{3,2,1,0:T(8,128)(2,1)} %a_hbm.1, bf16[1,4,4096,2816]{3,2,1,0:T(8,128)(2,1)} %g_hbm.1), custom_call_target="tpu_custom_call" | custom-call | flops 94489280512 | bytes 125829120 | tf_op jit(solution)/shard_map/multiply_and_sum/pallas_call | solution.py:307
  202.0 8.1 %place.1 = bf16[4,1024,2816]{2,1,0:T(8,128)(2,1)} custom-call(bf16[44,1024,256]{2,1,0:T(8,128)(2,1)S(1)} %multiply_and_sum.1.sums), custom_call_target="tpu_custom_call" | custom-call | tf_op jit(solution)/shard_map/place/pallas_call | solution.py:338
